TPU v7x, 32 devices: a 4x4x1 block of a 4x4x8 slice. The times are simulated.
32 devices in a mesh: rep: 1 (over z), data: 32 (over y, x, core).
Axes of the slice: x: 4, y: 4, z: 1, core: 2. Of those that a mesh axis runs over, the one named last changes fastest.
The devices are a block of a 4x4x8 slice.
Arguments:
- x: bfloat16 [2048, 3072], P(('rep', 'data'))
- adapter_id: int32 [2048], P(('rep', 'data'))
- w_gate: bfloat16 [3072, 8192], replicated
- w_up: bfloat16 [3072, 8192], replicated
- w_down: bfloat16 [8192, 3072], replicated
- a_gate: bfloat16 [256, 16, 3072], P('data')
- b_gate: bfloat16 [256, 16, 8192], P('data')
- a_up: bfloat16 [256, 16, 3072], P('data')
- b_up: bfloat16 [256, 16, 8192], P('data')
- a_down: bfloat16 [256, 16, 8192], P('data')
- b_down: bfloat16 [256, 16, 3072], P('data')
Outputs:
- output: bfloat16 [2048, 3072], P(('rep', 'data'))
All inputs are finite; a program needn't handle non-finite values.
Results may differ from a plain program's by a relative error of at most 0.00573171.
Values are sent between devices in bfloat16 or wider.
A program may use at most 768 MiB of HBM per device.

v0:
```python
import jax
import jax.numpy as jnp
from jax import lax
from jax.sharding import PartitionSpec as P

LORA_ALPHA = 32


def solution(mesh):
    groups = mesh.shape["data"]
    row_spec = P(("rep", "data"), None)
    id_spec = P(("rep", "data"))
    owned_spec = P("data", None, None)

    def device_step(x, adapter_id, w_gate, w_up, w_down, a_gate, b_gate, a_up, b_up, a_down, b_down):
        tok, dim = x.shape
        per_owner, rank, _ = a_gate.shape
        scale = LORA_ALPHA / rank
        cap = (3 * tok + groups - 1) // groups
        stack = per_owner * rank
        owner = adapter_id // per_owner
        local = adapter_id % per_owner
        owner_hot = (owner[:, None] == jnp.arange(groups)[None, :]).astype(jnp.int32)
        arrival = jnp.sum(jnp.cumsum(owner_hot, axis=0) * owner_hot, axis=1) - 1
        slot = owner * cap + arrival
        dispatch = (slot[:, None] == jnp.arange(groups * cap)[None, :]).astype(jnp.bfloat16)
        mine = (local[:, None] == (jnp.arange(stack) // rank)[None, :]).astype(jnp.bfloat16)
        rows = jnp.concatenate([x, mine], axis=1)
        send = jnp.einsum("tm,td->md", dispatch, rows, preferred_element_type=jnp.float32).astype(jnp.bfloat16)
        recv = lax.all_to_all(send, "data", 0, 0, tiled=True)
        xr, keep = recv[:, :dim], recv[:, dim:] > 0

        def delta(v, a, b):
            low = jnp.einsum("md,rd->mr", v, a.reshape(stack, -1), preferred_element_type=jnp.float32)
            low = jnp.where(keep, low.astype(jnp.bfloat16), jnp.bfloat16(0))
            full = jnp.dot(low, b.reshape(stack, -1), preferred_element_type=jnp.float32)
            return (scale * full).astype(jnp.bfloat16).astype(jnp.float32)

        gate = jnp.dot(xr, w_gate, preferred_element_type=jnp.float32) + delta(xr, a_gate, b_gate)
        up = jnp.dot(xr, w_up, preferred_element_type=jnp.float32) + delta(xr, a_up, b_up)
        hidden = (jax.nn.silu(gate) * up).astype(jnp.bfloat16)
        down = jnp.dot(hidden, w_down, preferred_element_type=jnp.float32) + delta(hidden, a_down, b_down)
        out = (xr.astype(jnp.float32) + down).astype(jnp.bfloat16)
        back = lax.all_to_all(out, "data", 0, 0, tiled=True)
        return jnp.einsum("tm,md->td", dispatch, back, preferred_element_type=jnp.float32).astype(jnp.bfloat16)

    return jax.shard_map(device_step, mesh=mesh, in_specs=(row_spec, id_spec, P(), P(), P(), owned_spec, owned_spec, owned_spec, owned_spec, owned_spec, owned_spec), out_specs=row_spec, check_vma=False)
```

profile of v0, /device:TPU:97, one launch (start us, length us, event | category | flops | bytes accessed | tf_op | source)
XLA Modules:
  0.0 157.7 jit_solution(2951100945296611389)
XLA Ops:
  0.0 0.0 copy-start
  0.0 0.8 and_select_fusion.2
  0.8 0.1 fusion.24
  0.9 0.1 reduce_window_sum.11
  1.0 0.2 select_reduce_fusion
  1.2 0.1 compare_convert_fusion
  1.3 1.6 %convolution_convert_fusion = bf16[192,3200]{1,0:T(8,128)(2,1)S(1)} fusion(bf16[64,128]{1,0:T(8,128)(2,1)S(1)} %compare_convert_fusion, bf16[64,3072]{1,0:T(8,128)(2,1)} %param.11, s32[64]{0:T(128)S(1)} %add_add_fusion), kind=kOutput, calls=%fused_computation.10 | convolution fusion | flops 80089088 | bytes 1638656 | tf_op jit(solution)/shard_map/tm,td->md/dot_general | solution.py:29
  2.9 1.4 all_to_all.16
  4.3 33.2 %all_to_all.24 = bf16[32,6,3200]{2,1,0:T(8,128)(2,1)} all-to-all(bf16[32,6,3200]{2,1,0:T(8,128)(2,1)} %all_to_all.16), channel_id=1, replica_groups=mesh['rep'=1,'data'=32] {'data'}, dimensions={0} | all-to-all | bytes 2457600 | tf_op jit(solution)/shard_map/all_to_all | solution.py:30
  37.5 2.4 %all_to_all.18 = bf16[192,3200]{1,0:T(8,128)(2,1)S(1)} reshape(bf16[32,6,3200]{2,1,0:T(8,128)(2,1)} %all_to_all.24) | data formatting | bytes 2457600 | tf_op jit(solution)/shard_map/all_to_all | solution.py:30
  39.8 0.0 copy-done
  39.9 5.8 %fusion.5 = f32[192,8192]{1,0:T(8,128)} fusion(bf16[128,8192]{1,0:T(8,128)(2,1)S(1)} %bitcast.18, bf16[128,3072]{1,0:T(8,128)(2,1)} %bitcast.21, bf16[192,3200]{1,0:T(8,128)(2,1)S(1)} %all_to_all.18), kind=kOutput, calls=%fused_computation.9 | convolution fusion | flops 558440448 | bytes 10403840 | tf_op jit(solution)/shard_map/dot_general | solution.py:36
  45.6 0.0 copy-start.2
  45.6 24.5 %convolution_add_fusion.1 = f32[192,8192]{1,0:T(8,128)} fusion(f32[192,8192]{1,0:T(8,128)} %fusion.5, bf16[3072,8192]{1,0:T(8,128)(2,1)} %param.13, bf16[192,3200]{1,0:T(8,128)(2,1)S(1)} %all_to_all.18), kind=kOutput, calls=%fused_computation.4 | convolution fusion | flops 9665249280 | bytes 64094208 | tf_op jit(solution)/shard_map/dot_general | solution.py:39
  70.1 0.0 copy-done.2
  70.1 5.8 %fusion.4 = f32[192,8192]{1,0:T(8,128)} fusion(bf16[128,8192]{1,0:T(8,128)(2,1)S(1)} %bitcast.19, bf16[128,3072]{1,0:T(8,128)(2,1)} %bitcast.22, bf16[192,3200]{1,0:T(8,128)(2,1)S(1)} %all_to_all.18), kind=kOutput, calls=%fused_computation.8 | convolution fusion | flops 558440448 | bytes 10403840 | tf_op jit(solution)/shard_map/dot_general | solution.py:36
  75.9 0.0 copy-start.3
  75.9 24.7 %fusion.1 = bf16[192,8192]{1,0:T(8,128)(2,1)} fusion(f32[192,8192]{1,0:T(8,128)} %fusion.4, bf16[3072,8192]{1,0:T(8,128)(2,1)} %param.14, f32[192,8192]{1,0:T(8,128)} %convolution_add_fusion.1, bf16[192,3200]{1,0:T(8,128)(2,1)S(1)} %all_to_all.18), kind=kOutput, calls=%fused_computation.5 | convolution fusion | flops 9674686464 | bytes 67239936 | tf_op jit(solution)/shard_map/dot_general | solution.py:40
  100.6 0.0 copy-done.3
  100.6 5.4 %fusion.8 = f32[192,3072]{1,0:T(8,128)} fusion(bf16[128,3072]{1,0:T(8,128)(2,1)} %bitcast.23, bf16[192,8192]{1,0:T(8,128)(2,1)} %fusion.1, bf16[128,8192]{1,0:T(8,128)(2,1)S(1)} %bitcast.20, bf16[192,3200]{1,0:T(8,128)(2,1)S(1)} %all_to_all.18), kind=kOutput, calls=%fused_computation.15 | convolution fusion | flops 555491328 | bytes 8437760 | tf_op jit(solution)/shard_map/dot_general | solution.py:36
  106.1 20.5 %fusion.9 = bf16[192,3072]{1,0:T(8,128)(2,1)S(1)} fusion(f32[192,3072]{1,0:T(8,128)} %fusion.8, bf16[192,8192]{1,0:T(8,128)(2,1)} %fusion.1, bf16[8192,3072]{1,0:T(8,128)(2,1)} %param.15, bf16[192,3200]{1,0:T(8,128)(2,1)S(1)} %all_to_all.18), kind=kOutput, calls=%fused_computation.16 | convolution fusion | flops 9666035712 | bytes 58195968 | tf_op jit(solution)/shard_map/dot_general | solution.py:42
  126.6 1.4 all_to_all.19
  128.0 0.0 copy-start.1
  128.0 27.0 %all_to_all.25 = bf16[32,6,3072]{2,1,0:T(8,128)(2,1)} all-to-all(bf16[32,6,3072]{2,1,0:T(8,128)(2,1)} %all_to_all.19), channel_id=1, replica_groups=mesh['rep'=1,'data'=32] {'data'}, dimensions={0} | all-to-all | bytes 2359296 | tf_op jit(solution)/shard_map/all_to_all | solution.py:44
  155.0 1.6 %all_to_all.21 = bf16[192,3072]{1,0:T(8,128)(2,1)S(1)} reshape(bf16[32,6,3072]{2,1,0:T(8,128)(2,1)} %all_to_all.25) | data formatting | bytes 2359296 | tf_op jit(solution)/shard_map/all_to_all | solution.py:44
  156.6 1.1 convolution_convert_fusion.1
  157.7 0.0 copy-done.1
  (2 shorter events, 0.0 us)
Async XLA Ops:
  0.0 39.8 %copy-start = (bf16[8,16,8192]{2,1,0:T(8,128)(2,1)S(1)}, bf16[8,16,8192]{2,1,0:T(8,128)(2,1)}, u32[]{:S(2)}) copy-start(bf16[8,16,8192]{2,1,0:T(8,128)(2,1)} %param.17) | copy-start | bytes 6291460
  45.6 24.5 %copy-start.2 = (bf16[8,16,8192]{2,1,0:T(8,128)(2,1)S(1)}, bf16[8,16,8192]{2,1,0:T(8,128)(2,1)}, u32[]{:S(2)}) copy-start(bf16[8,16,8192]{2,1,0:T(8,128)(2,1)} %param.19) | copy-start | bytes 6291460
  75.9 24.7 %copy-start.3 = (bf16[8,16,8192]{2,1,0:T(8,128)(2,1)S(1)}, bf16[8,16,8192]{2,1,0:T(8,128)(2,1)}, u32[]{:S(2)}) copy-start(bf16[8,16,8192]{2,1,0:T(8,128)(2,1)} %param.20) | copy-start | bytes 6291460
  128.0 29.8 %copy-start.1 = (bf16[8,16,8192]{2,1,0:T(8,128)(2,1)S(1)}, bf16[8,16,8192]{2,1,0:T(8,128)(2,1)}, u32[]{:S(2)}) copy-start(bf16[8,16,8192]{2,1,0:T(8,128)(2,1)} %param.17) | copy-start | bytes 6291460
where the time goes:
time: 158 us
  matrix products  89.4 us (57%)
  blocking collectives  60.2 us (38%)
  local copies, waits for them, and re-layouts  6.74 us (4%)
    all_to_all x1, blocking collectives, device_step(): recv = lax.all_to_all(send, 'data', 0, 0, tiled=True)  33.2 us
    all_to_all x1, blocking collectives, device_step(): back = lax.all_to_all(out, 'data', 0, 0, tiled=True)  27 us
    dot_general x1, matrix products, device_step(): jnp.dot(xr, w_up, preferred_element_type=jnp.float32)  24.7 us
    dot_general x1, matrix products, device_step(): jnp.dot(xr, w_gate, preferred_element_type=jnp.float32)  24.5 us
    dot_general x1, matrix products, device_step(): jnp.dot(hidden, w_down, preferred_element_type=jnp.float32)  20.5 us
    dot_general x3, matrix products, delta(): jnp.dot(low, b.reshape(stack, -1), preferred_element_type=jnp.float32)  17 us
    all_to_all x2, local copies, waits for them, and re-layouts, device_step(): recv = lax.all_to_all(send, 'data', 0, 0, tiled=True)  3.78 us

commit v1 on v0

v1 whole, which is shorter than its diff:
```python
import functools
import math

import jax
import jax.numpy as jnp
from jax import lax
from jax.experimental import pallas as pl
from jax.experimental.pallas import tpu as pltpu
from jax.sharding import PartitionSpec as P

LORA_ALPHA = 32
BF, F32 = jnp.bfloat16, jnp.float32
CORES = 2
UNIT_K, UNIT_N = 1024, 512
UNITS = 36
MAIN = 384


def one_hot(rows, cols, hit):
    r = lax.broadcasted_iota(jnp.int32, (rows, cols), 0)
    c = lax.broadcasted_iota(jnp.int32, (rows, cols), 1)
    return hit(r, c).astype(F32).astype(BF)


def dot(a, b):
    return jnp.dot(a, b, preferred_element_type=F32)


def dot_t(a, b):
    return lax.dot_general(a, b, (((1,), (1,)), ((), ())), preferred_element_type=F32)


def layer(groups, cap, scale, rank, ids_ref, x_hbm, wg_hbm, wu_hbm, wd_hbm, ag_hbm, bg_hbm, au_hbm, bu_hbm, ad_hbm, bd_hbm, out_hbm,
          ring, x_v, xc, h_v, agu, bgu, adv, bdv, send1, recv1, send2, recv2, o_v, keep_v, low_v, gmat,
          ring_sem, in_sem, s1_sem, r1_sem, s2_sem, r2_sem):
    tok, dim = x_v.shape
    ff = h_v.shape[1]
    stack = bdv.shape[0]
    slots = groups * cap
    slab = send1.shape[1]
    packed = groups * slab
    side = math.isqrt(groups // CORES)
    n_in = ff // UNIT_N
    k_in = dim // UNIT_K
    n_out = dim // UNIT_N
    k_out = ff // UNIT_K
    in_units = n_in * 2 * k_in
    me = lax.axis_index("data")
    my_c, my_x, my_y = lax.rem(me, CORES), lax.rem(me // CORES, side), me // (CORES * side)

    def target(r, back=False):
        dy, dx, dc = r // (CORES * side), (r // CORES) % side, r % CORES
        if back:
            dy, dx = (side - dy) % side, (side - dx) % side
        return {"data": (lax.rem(my_y + dy, side) * side + lax.rem(my_x + dx, side)) * CORES + lax.rem(my_c + dc, CORES)}

    def in_copy(src, dst, i):
        return pltpu.make_async_copy(src, dst, in_sem.at[i])

    def in_unit(j, which, k, slot):
        src = (wg_hbm, wu_hbm)[which]
        col = pl.multiple_of(j * UNIT_N, UNIT_N)
        return pltpu.make_async_copy(src.at[pl.ds(k * UNIT_K, UNIT_K), pl.ds(col, UNIT_N)], ring.at[slot], ring_sem.at[slot])

    def out_unit(n, k, slot):
        col = pl.multiple_of(n * UNIT_N, UNIT_N)
        row = pl.multiple_of(k * UNIT_K, UNIT_K)
        return pltpu.make_async_copy(wd_hbm.at[pl.ds(row, UNIT_K), pl.ds(col, UNIT_N)], ring.at[slot], ring_sem.at[slot])

    half = agu.shape[0] // 2
    x_copy = in_copy(x_hbm, x_v, 0)
    x_copy.start()
    early = [in_copy(ag_hbm, agu.at[pl.ds(0, half)], 1), in_copy(au_hbm, agu.at[pl.ds(half, half)], 2),
             in_copy(bg_hbm, bgu.at[0], 3), in_copy(bu_hbm, bgu.at[1], 4)]
    late = [in_copy(ad_hbm, adv, 5), in_copy(bd_hbm, bdv, 6)]
    for c in early:
        c.start()
    per = 2 * k_in
    for u in range(UNITS):
        in_unit(u // per, (u % per) // k_in, u % k_in, u).start()
    for c in late:
        c.start()

    barrier = pltpu.get_barrier_semaphore()
    for r in range(1, groups):
        pl.semaphore_signal(barrier, inc=1, device_id=target(r), device_id_type=pl.DeviceIdType.MESH)

    ids = ids_ref[...].astype(F32)
    eye = lax.broadcasted_iota(jnp.int32, (tok, tok), 0) == lax.broadcasted_iota(jnp.int32, (tok, tok), 1)
    ids_c = jnp.sum(jnp.where(eye, jnp.broadcast_to(ids, (tok, tok)), 0.0), axis=1, keepdims=True)
    per_owner = stack // rank

    def fdiv(v, n):
        return jnp.floor((v + 0.5) * (1.0 / n))

    def place(v):
        owner = fdiv(v, per_owner)
        local = v - owner * per_owner
        oy = fdiv(owner, CORES * side)
        ox = fdiv(owner, CORES) - oy * side
        oc = owner - fdiv(owner, CORES) * CORES

        def mod(a, b, n):
            d = a - b.astype(F32)
            return jnp.where(d < 0, d + n, d)
        rel = (mod(oy, my_y, side) * side + mod(ox, my_x, side)) * CORES + mod(oc, my_c, CORES)
        return owner, local, rel

    own_r, _, rel_r = place(ids)
    own_c, loc_c, rel_c = place(ids_c)
    t0 = lax.broadcasted_iota(jnp.int32, (tok, tok), 0)
    t1 = lax.broadcasted_iota(jnp.int32, (tok, tok), 1)
    same = own_c == own_r
    arr_r = jnp.sum(jnp.where(same & (t0 < t1), 1.0, 0.0), axis=0, keepdims=True)
    arr_c = jnp.sum(jnp.where(same & (t1 < t0), 1.0, 0.0), axis=1, keepdims=True)
    third = cap // 2

    def rows_of(rel, arr):
        main = (rel * slab + arr).astype(jnp.int32)
        tail_row = fdiv(arr, third)
        tail = (rel * slab + cap + tail_row).astype(jnp.int32)
        part = (arr - tail_row * third).astype(jnp.int32)
        return main, tail, part

    main_r, tail_r, part_r = rows_of(rel_r, arr_r)
    main_c, tail_c, part_c = rows_of(rel_c, arr_c)
    s_main = one_hot(packed, tok, lambda r, c: r == main_r)
    s_tail = [one_hot(packed, tok, lambda r, c: (r == tail_r) & (part_r == k)) for k in range(third)]
    gmat[0] = one_hot(tok, packed, lambda r, c: c == main_c)
    for k in range(third):
        gmat[1 + k] = one_hot(tok, packed, lambda r, c: (c == tail_c) & (part_c == k))
    mine = one_hot(tok, stack, lambda r, c: loc_c == fdiv(c.astype(F32), rank))

    x_copy.wait()
    mask0 = n_out * MAIN
    for n in range(n_out):
        xa = x_v[:, n * UNIT_N:n * UNIT_N + MAIN]
        xb = x_v[:, n * UNIT_N + MAIN:(n + 1) * UNIT_N]
        both = dot(s_main, xa) + jnp.concatenate([dot(s, xb) for s in s_tail], axis=1)
        send1[:, :, n * MAIN:(n + 1) * MAIN] = both.reshape(groups, slab, MAIN).astype(BF)
    send1[:, :, mask0:] = dot(s_main, mine).reshape(groups, slab, stack).astype(BF)

    pl.semaphore_wait(barrier, groups - 1)

    def copy1(r):
        return pltpu.make_async_remote_copy(send1.at[r], recv1.at[r], s1_sem.at[r], r1_sem.at[r], device_id=target(r), device_id_type=pl.DeviceIdType.MESH)

    for r in range(1, groups):
        copy1(r).start()
    recv1[0] = send1[0]

    def slot_of(s):
        g = fdiv(s.astype(F32), cap).astype(jnp.int32)
        return g, s - g * cap

    def unpack_main(r, c):
        g, j = slot_of(r)
        return c == g * slab + j

    def unpack_tail(k):
        def hit(r, c):
            g, j = slot_of(r)
            q = fdiv(j.astype(F32), third).astype(jnp.int32)
            return (c == g * slab + cap + q) & (j - q * third == k)
        return hit

    def pack_main(r, c):
        return unpack_main(c, r)

    def pack_tail(k):
        def hit(r, c):
            return unpack_tail(k)(c, r)
        return hit

    p_main = one_hot(slots, packed, unpack_main)
    p_tail = [one_hot(slots, packed, unpack_tail(k)) for k in range(third)]

    def lanes(ref, at, width):
        return ref[:, :, at:at + width].astype(F32).reshape(packed, width).astype(BF)

    for r in range(1, groups):
        copy1(r).wait()
    for n in range(n_out):
        part = lanes(recv1, n * MAIN, MAIN)
        xc[:, n * UNIT_N:n * UNIT_N + MAIN] = dot(p_main, part).astype(BF)
        w = MAIN // third
        tail = sum(dot(p_tail[k], part[:, k * w:(k + 1) * w]) for k in range(third))
        xc[:, n * UNIT_N + MAIN:(n + 1) * UNIT_N] = tail.astype(BF)
    keep_v[...] = dot(p_main, lanes(recv1, mask0, stack))

    for c in early:
        c.wait()
    keep = keep_v[...] > 0.5
    low = dot_t(xc[...], agu[...])
    for i in range(2):
        low_v[i] = jnp.where(keep, low[:, i * stack:(i + 1) * stack].astype(BF).astype(F32), 0.0).astype(BF)

    blocks = 2
    step_units = blocks * per

    def in_step(i, carry):
        base = i * step_units
        for k in range(step_units):
            slot = lax.rem(base + k, UNITS)
            in_unit(0, 0, 0, slot).wait()
        for b in range(blocks):
            j = i * blocks + b
            for s in range(UNIT_N // 256):
                res = []
                for which in range(2):
                    acc = None
                    for k in range(k_in):
                        slot = lax.rem(base + b * per + which * k_in + k, UNITS)
                        d = dot(xc[:, k * UNIT_K:(k + 1) * UNIT_K], ring[slot, :, s * 256:(s + 1) * 256])
                        acc = d if acc is None else acc + d
                    col = pl.multiple_of(j * UNIT_N + s * 256, 256)
                    delta = (scale * dot(low_v[which], bgu[which, :, pl.ds(col, 256)])).astype(BF).astype(F32)
                    res.append(acc + delta)
                g, u = res
                h_v[:, pl.ds(col, 256)] = (g * (1.0 / (1.0 + jnp.exp(-g))) * u).astype(BF)
        nxt = base + UNITS

        @pl.when(nxt < in_units)
        def _():
            for k in range(step_units):
                in_unit(lax.div(nxt, per) + k // per, (k % per) // k_in, k % k_in, lax.rem(base + k, UNITS)).start()

        @pl.when(nxt >= in_units)
        def _():
            for k in range(step_units):
                v = nxt - in_units + k
                out_unit(lax.div(v, k_out), lax.rem(v, k_out), lax.rem(base + k, UNITS)).start()
        return carry

    lax.fori_loop(0, n_in // blocks, in_step, 0)

    for c in late:
        c.wait()
    low = dot_t(h_v[...], adv[...])
    low_v[0] = jnp.where(keep_v[...] > 0.5, low.astype(BF).astype(F32), 0.0).astype(BF)
    e_main = one_hot(packed, slots, pack_main)
    e_tail = [one_hot(packed, slots, pack_tail(k)) for k in range(third)]

    def copy2(n, r):
        return pltpu.make_async_remote_copy(send2.at[n, r], recv2.at[n, r], s2_sem.at[n, r], r2_sem.at[n, r], device_id=target(r, True), device_id_type=pl.DeviceIdType.MESH)

    total = in_units + n_out * k_out
    for n in range(n_out):
        base = in_units + n * k_out
        for k in range(k_out):
            out_unit(n, k, (base + k) % UNITS).wait()
        cols = slice(n * UNIT_N, (n + 1) * UNIT_N)
        acc = None
        for k in range(k_out):
            d = dot(h_v[:, k * UNIT_K:(k + 1) * UNIT_K], ring[(base + k) % UNITS])
            acc = d if acc is None else acc + d
        delta = (scale * dot(low_v[0], bdv[:, cols])).astype(BF).astype(F32)
        done = (xc[:, cols].astype(F32) + (acc + delta)).astype(BF)
        both = dot(e_main, done[:, :MAIN]) + jnp.concatenate([dot(e, done[:, MAIN:]) for e in e_tail], axis=1)
        send2[n] = both.reshape(groups, slab, MAIN).astype(BF)
        for r in range(1, groups):
            copy2(n, r).start()
        recv2[n, 0] = send2[n, 0]
        for k in range(k_out):
            u = base + k + UNITS
            if u < total:
                out_unit((u - in_units) // k_out, (u - in_units) % k_out, u % UNITS).start()

    for n in range(n_out):
        for r in range(1, groups):
            copy2(n, r).wait()
        part = recv2[n].astype(F32).reshape(packed, MAIN).astype(BF)
        w = MAIN // third
        o_v[:, n * UNIT_N:n * UNIT_N + MAIN] = dot(gmat[0], part).astype(BF)
        tail = sum(dot(gmat[1 + k], part[:, k * w:(k + 1) * w]) for k in range(third))
        o_v[:, n * UNIT_N + MAIN:(n + 1) * UNIT_N] = tail.astype(BF)
    last = in_copy(o_v, out_hbm, 7)
    last.start()
    last.wait()


def solution(mesh):
    groups = mesh.shape["data"]
    row_spec = P(("rep", "data"), None)
    id_spec = P(("rep", "data"))
    owned_spec = P("data", None, None)

    def device_step(x, adapter_id, w_gate, w_up, w_down, a_gate, b_gate, a_up, b_up, a_down, b_down):
        tok, dim = x.shape
        ff = w_gate.shape[1]
        per_owner, rank, _ = a_gate.shape
        stack = per_owner * rank
        cap = (3 * tok + groups - 1) // groups
        slots = groups * cap
        slab = 8
        n_out = dim // UNIT_N
        width = n_out * MAIN + stack
        flat = [m.reshape(stack, m.shape[2]) for m in (a_gate, b_gate, a_up, b_up, a_down, b_down)]
        anyspec = pl.BlockSpec(memory_space=pl.ANY)
        dma = pltpu.SemaphoreType.DMA
        return pl.pallas_call(
            functools.partial(layer, groups, cap, LORA_ALPHA / rank, rank),
            out_shape=jax.ShapeDtypeStruct((tok, dim), BF),
            in_specs=[pl.BlockSpec(memory_space=pltpu.VMEM)] + [anyspec] * 10,
            out_specs=anyspec,
            scratch_shapes=[
                pltpu.VMEM((UNITS, UNIT_K, UNIT_N), BF),
                pltpu.VMEM((tok, dim), BF),
                pltpu.VMEM((slots, dim), BF),
                pltpu.VMEM((slots, ff), BF),
                pltpu.VMEM((2 * stack, dim), BF),
                pltpu.VMEM((2, stack, ff), BF),
                pltpu.VMEM((stack, ff), BF),
                pltpu.VMEM((stack, dim), BF),
                pltpu.VMEM((groups, slab, width), BF),
                pltpu.VMEM((groups, slab, width), BF),
                pltpu.VMEM((n_out, groups, slab, MAIN), BF),
                pltpu.VMEM((n_out, groups, slab, MAIN), BF),
                pltpu.VMEM((tok, dim), BF),
                pltpu.VMEM((slots, stack), F32),
                pltpu.VMEM((2, slots, stack), BF),
                pltpu.VMEM((1 + cap // 2, tok, groups * slab), BF),
                dma((UNITS,)), dma((8,)), dma((groups,)), dma((groups,)), dma((n_out, groups)), dma((n_out, groups)),
            ],
            compiler_params=pltpu.CompilerParams(collective_id=0, has_side_effects=True, vmem_limit_bytes=67043328),
            name="lora_swiglu",
        )(adapter_id.reshape(1, tok), x, w_gate, w_up, w_down, *flat)

    return jax.shard_map(device_step, mesh=mesh, in_specs=(row_spec, id_spec, P(), P(), P(), owned_spec, owned_spec, owned_spec, owned_spec, owned_spec, owned_spec), out_specs=row_spec, check_vma=False)
```

time: 158 us -> 104 us (0.66)
  Pallas kernels: 0 us -> 102 us
  matrix products: 89.4 us -> 0 us
  blocking collectives: 60.2 us -> 0 us
  local copies, waits for them, and re-layouts: 6.74 us -> 1.77 us
    pallas_call x0 -> x1, Pallas kernels: none -> 102 us  [device_step(): pl.pallas_call(functools.partial(layer, groups, cap, LORA_ALPHA / rank, r...]
    dot_general x8 -> x0, matrix products: 89.4 us -> none  [the longest x1 24.7 us: device_step(): jnp.dot(xr, w_up, preferred_element_type=jnp.float32)]
    all_to_all x2 -> x0, blocking collectives: 60.2 us -> none  [the longest x1 33.2 us: device_step(): recv = lax.all_to_all(send, 'data', 0, 0, tiled=True)]
    all_to_all x4 -> x0, local copies, waits for them, and re-layouts: 6.73 us -> none  [the longest x2 3.78 us: device_step(): recv = lax.all_to_all(send, 'data', 0, 0, tiled=True)]
    unnamed x8 -> x1, local copies, waits for them, and re-layouts: 0.02 us -> 1.77 us
where the time goes in v1:
time: 104 us
  Pallas kernels  102 us (98%)
  local copies, waits for them, and re-layouts  1.77 us (2%)
    pallas_call x1, Pallas kernels, device_step(): pl.pallas_call(functools.partial(layer, groups, cap, LORA_ALPHA / rank, r...  102 us

profile of v1, /device:TPU:97, one launch (start us, length us, event | category | flops | bytes accessed | tf_op | source)
XLA Modules:
  0.0 103.5 jit_solution(17434926337219956404)
XLA Ops:
  0.0 101.8 %lora_swiglu.1 = bf16[64,3072]{1,0:T(8,128)(2,1)} custom-call(s32[1,64]{1,0:T(1,128)} %bitcast.13, bf16[64,3072]{1,0:T(8,128)(2,1)} %x_hbm.1, bf16[3072,8192]{1,0:T(8,128)(2,1)} %wg_hbm.1, bf16[3072,8192]{1,0:T(8,128)(2,1)} %wu_hbm.1, bf16[8192,3072]{1,0:T(8,128)(2,1)} %wd_hbm.1, bf16[128,3072]{1,0:T(8,128)(2,1)} %bitcast.10, bf16[128,8192]{1,0:T(8,128)(2,1)} %bitcast.7, ...), custom_call_target="tpu_custom_call" | custom-call | tf_op jit(solution)/shard_map/lora_swiglu/pallas_call | solution.py:301
  101.8 1.8 %copy.13 = bf16[64,3072]{1,0:T(8,128)(2,1)} copy(bf16[64,3072]{1,0:T(8,128)(2,1)} %lora_swiglu.1) | data formatting | bytes 786432

commit v2 on v0

v2 whole, which is shorter than its diff:
```python
import functools
import math

import jax
import jax.numpy as jnp
from jax import lax
from jax.experimental import pallas as pl
from jax.experimental.pallas import tpu as pltpu
from jax.sharding import PartitionSpec as P

LORA_ALPHA = 32
BF, F32 = jnp.bfloat16, jnp.float32
CORES = 2
UNIT_K, UNIT_N = 1024, 512
UNITS = 32
MAIN = 384


def one_hot(rows, cols, hit):
    r = lax.broadcasted_iota(jnp.int32, (rows, cols), 0)
    c = lax.broadcasted_iota(jnp.int32, (rows, cols), 1)
    return hit(r, c).astype(F32).astype(BF)


def dot(a, b):
    return jnp.dot(a, b, preferred_element_type=F32)


def dot_t(a, b):
    return lax.dot_general(a, b, (((1,), (1,)), ((), ())), preferred_element_type=F32)


def layer(groups, cap, scale, rank, ids_ref, x_hbm, wg_hbm, wu_hbm, wd_hbm, ag_hbm, bg_hbm, au_hbm, bu_hbm, ad_hbm, bd_hbm, out_hbm,
          ring, acc_v, x_v, xc, h_v, bgu, adv, bdv, send0, recv0, send1, recv1, recv2, keep_v, low_v, gmat,
          ring_sem, in_sem, s1_sem, r1_sem, s2_sem, r2_sem):
    tok, dim = x_v.shape
    ff = h_v.shape[1]
    stack = bdv.shape[0]
    slots = groups * cap
    slab = recv0.shape[1]
    packed = groups * slab
    side = math.isqrt(groups // CORES)
    third = cap // 2
    n_in = ff // UNIT_N
    k_in = dim // UNIT_K
    n_out = dim // UNIT_N
    k_out = ff // UNIT_K
    chunks = UNIT_K // UNIT_N
    me = lax.axis_index("data")
    my_c, my_x, my_y = lax.rem(me, CORES), lax.rem(me // CORES, side), me // (CORES * side)

    def target(r, back=False):
        dy, dx, dc = r // (CORES * side), (r // CORES) % side, r % CORES
        if back:
            dy, dx = (side - dy) % side, (side - dx) % side
        return {"data": (lax.rem(my_y + dy, side) * side + lax.rem(my_x + dx, side)) * CORES + lax.rem(my_c + dc, CORES)}

    def in_copy(src, dst, i):
        return pltpu.make_async_copy(src, dst, in_sem.at[i])

    def in_unit(kk, j, which, slot):
        src = (wg_hbm, wu_hbm)[which]
        col = pl.multiple_of(j * UNIT_N, UNIT_N)
        return pltpu.make_async_copy(src.at[pl.ds(kk * UNIT_K, UNIT_K), pl.ds(col, UNIT_N)], ring.at[slot], ring_sem.at[slot])

    def out_unit(n, k, slot):
        col = pl.multiple_of(n * UNIT_N, UNIT_N)
        return pltpu.make_async_copy(wd_hbm.at[pl.ds(k * UNIT_K, UNIT_K), pl.ds(col, UNIT_N)], ring.at[slot], ring_sem.at[slot])

    x_copy = in_copy(x_hbm, x_v, 0)
    x_copy.start()
    early = [in_copy(ag_hbm, h_v.at[pl.ds(0, stack), pl.ds(0, dim)], 1), in_copy(au_hbm, h_v.at[pl.ds(0, stack), pl.ds(dim, dim)], 2),
             in_copy(bg_hbm, bgu.at[0], 3), in_copy(bu_hbm, bgu.at[1], 4)]
    late = [in_copy(ad_hbm, adv, 5), in_copy(bd_hbm, bdv, 6)]
    first = 4
    for u in range(first):
        in_unit(0, u // 2, u % 2, u).start()

    with jax.named_scope("signal"):
        barrier = pltpu.get_barrier_semaphore()
        for r in range(1, groups):
            pl.semaphore_signal(barrier, inc=1, device_id=target(r), device_id_type=pl.DeviceIdType.MESH)

    with jax.named_scope("place"):
        ids = ids_ref[...].astype(F32)
        eye = lax.broadcasted_iota(jnp.int32, (tok, tok), 0) == lax.broadcasted_iota(jnp.int32, (tok, tok), 1)
        ids_c = jnp.sum(jnp.where(eye, jnp.broadcast_to(ids, (tok, tok)), 0.0), axis=1, keepdims=True)
        per_owner = stack // rank

        def fdiv(v, n):
            return jnp.floor((v + 0.5) * (1.0 / n))

        def place(v):
            owner = fdiv(v, per_owner)
            local = v - owner * per_owner
            oy = fdiv(owner, CORES * side)
            ox = fdiv(owner, CORES) - oy * side
            oc = owner - fdiv(owner, CORES) * CORES

            def mod(a, b, n):
                d = a - b.astype(F32)
                return jnp.where(d < 0, d + n, d)
            rel = (mod(oy, my_y, side) * side + mod(ox, my_x, side)) * CORES + mod(oc, my_c, CORES)
            return owner, local, rel

        own_r, _, rel_r = place(ids)
        own_c, loc_c, rel_c = place(ids_c)
        t0 = lax.broadcasted_iota(jnp.int32, (tok, tok), 0)
        t1 = lax.broadcasted_iota(jnp.int32, (tok, tok), 1)
        same = own_c == own_r
        arr_r = jnp.sum(jnp.where(same & (t0 < t1), 1.0, 0.0), axis=0, keepdims=True)
        arr_c = jnp.sum(jnp.where(same & (t1 < t0), 1.0, 0.0), axis=1, keepdims=True)

        def rows_of(rel, arr):
            main = (rel * slab + arr).astype(jnp.int32)
            tail_row = fdiv(arr, third)
            tail = (rel * slab + cap + tail_row).astype(jnp.int32)
            part = (arr - tail_row * third).astype(jnp.int32)
            return main, tail, part

        main_r, tail_r, part_r = rows_of(rel_r, arr_r)
        main_c, tail_c, part_c = rows_of(rel_c, arr_c)
        s_main = one_hot(packed, tok, lambda r, c: r == main_r)
        s_tail = [one_hot(packed, tok, lambda r, c: (r == tail_r) & (part_r == k)) for k in range(third)]
        gmat[0] = one_hot(tok, packed, lambda r, c: c == main_c)
        for k in range(third):
            gmat[1 + k] = one_hot(tok, packed, lambda r, c: (c == tail_c) & (part_c == k))
        mine = one_hot(tok, stack, lambda r, c: loc_c == fdiv(c.astype(F32), rank))

    with jax.named_scope("x_wait"):
        x_copy.wait()
    with jax.named_scope("weights"):
        for u in range(first, UNITS):
            in_unit(0, u // 2, u % 2, u).start()
        for c in early:
            c.start()
        for c in late:
            c.start()

    def sends(kk):
        return send0 if kk == 0 else send1.at[kk - 1]

    def recvs(kk):
        return recv0 if kk == 0 else recv1.at[kk - 1]

    def copy1(kk, r):
        return pltpu.make_async_remote_copy(sends(kk).at[r], recvs(kk).at[r], s1_sem.at[kk, r], r1_sem.at[kk, r], device_id=target(r), device_id_type=pl.DeviceIdType.MESH)

    mask0 = chunks * MAIN
    for kk in range(k_in):
        with jax.named_scope(f"pack{kk}"):
            for b in range(chunks):
                at = kk * UNIT_K + b * UNIT_N
                xa = x_v[:, at:at + MAIN]
                xb = x_v[:, at + MAIN:at + UNIT_N]
                both = dot(s_main, xa) + jnp.concatenate([dot(s, xb) for s in s_tail], axis=1)
                sends(kk)[:, :, b * MAIN:(b + 1) * MAIN] = both.reshape(groups, slab, MAIN).astype(BF)
            if kk == 0:
                send0[:, :, mask0:] = dot(s_main, mine).reshape(groups, slab, stack).astype(BF)
        if kk == 0:
            with jax.named_scope("bar_wait"):
                pl.semaphore_wait(barrier, groups - 1)
        with jax.named_scope(f"send{kk}"):
            for r in range(1, groups):
                copy1(kk, r).start()
            recvs(kk)[0] = sends(kk)[0]

    def slot_of(s):
        g = fdiv(s.astype(F32), cap).astype(jnp.int32)
        return g, s - g * cap

    def unpack_main(r, c):
        g, j = slot_of(r)
        return c == g * slab + j

    def unpack_tail(k):
        def hit(r, c):
            g, j = slot_of(r)
            q = fdiv(j.astype(F32), third).astype(jnp.int32)
            return (c == g * slab + cap + q) & (j - q * third == k)
        return hit

    def pack_main(r, c):
        return unpack_main(c, r)

    def pack_tail(k):
        def hit(r, c):
            return unpack_tail(k)(c, r)
        return hit

    with jax.named_scope("maps"):
        p_main = one_hot(slots, packed, unpack_main)
        p_tail = [one_hot(slots, packed, unpack_tail(k)) for k in range(third)]
    w = MAIN // third

    def lanes(ref, at, width):
        return ref[:, :, at:at + width].astype(F32).reshape(packed, width).astype(BF)

    def arrive(kk):
        with jax.named_scope(f"recv{kk}"):
            for r in range(1, groups):
                copy1(kk, r).wait()
        with jax.named_scope(f"unpack{kk}"):
            for b in range(chunks):
                at = kk * UNIT_K + b * UNIT_N
                part = lanes(recvs(kk), b * MAIN, MAIN)
                xc[:, at:at + MAIN] = dot(p_main, part).astype(BF)
                tail = sum(dot(p_tail[k], part[:, k * w:(k + 1) * w]) for k in range(third))
                xc[:, at + MAIN:at + UNIT_N] = tail.astype(BF)
            if kk == 0:
                keep_v[...] = dot(p_main, lanes(recv0, mask0, stack))

    def low_rank(v, a, i):
        low = dot_t(v, a)
        low_v[i] = jnp.where(keep_v[...] > 0.5, low.astype(BF).astype(F32), 0.0).astype(BF)

    blocks = 4
    per_step = 2 * blocks
    steps = n_in // blocks
    for kk in range(k_in):
        arrive(kk)
        if kk == k_in - 1:
            with jax.named_scope("low"):
                for c in early:
                    c.wait()
                for i in range(2):
                    low_rank(xc[...], h_v[0:stack, i * dim:(i + 1) * dim], i)

        def step(i, carry):
            base = i * per_step
            for k in range(per_step):
                in_unit(0, 0, 0, base + k).wait()
            with jax.named_scope(f"dot{kk}"):
                for b in range(blocks):
                    for s in range(UNIT_N // 256):
                        col = pl.ds(pl.multiple_of((i * blocks + b) * UNIT_N + s * 256, 256), 256)
                        res = []
                        for which in range(2):
                            d = dot(xc[:, kk * UNIT_K:(kk + 1) * UNIT_K], ring[base + b * 2 + which, :, s * 256:(s + 1) * 256])
                            if kk > 0:
                                d = acc_v[which, :, col] + d
                            if kk < k_in - 1:
                                acc_v[which, :, col] = d
                            else:
                                res.append(d + (scale * dot(low_v[which], bgu[which, :, col])).astype(BF).astype(F32))
                        if res:
                            g, u = res
                            h_v[:, col] = (g * (1.0 / (1.0 + jnp.exp(-g))) * u).astype(BF)
            for k in range(per_step):
                if kk < k_in - 1:
                    in_unit(kk + 1, i * blocks + k // 2, k % 2, base + k).start()
                else:
                    out_unit(i, k, base + k).start()
            return carry

        lax.fori_loop(0, steps, step, 0)

    with jax.named_scope("low2"):
        for c in late:
            c.wait()
        low_rank(h_v[...], adv[...], 0)
        e_main = one_hot(packed, slots, pack_main)
        e_tail = [one_hot(packed, slots, pack_tail(k)) for k in range(third)]

    def sent2(n):
        return send1.at[n % 2, :, :, pl.ds(n // 2 % chunks * MAIN, MAIN)]

    def copy2(n, r):
        return pltpu.make_async_remote_copy(sent2(n).at[r], recv2.at[n, r], s2_sem.at[n, r], r2_sem.at[n, r], device_id=target(r, True), device_id_type=pl.DeviceIdType.MESH)

    def ship(n):
        with jax.named_scope(f"ship{n}"):
            for r in range(1, groups):
                copy2(n, r).start()

    def home(n):
        with jax.named_scope(f"homewait{n}"):
            for r in range(1, groups):
                copy2(n, r).wait()
        with jax.named_scope(f"home{n}"):
            part = recv2[n].astype(F32).reshape(packed, MAIN).astype(BF)
            x_v[:, n * UNIT_N:n * UNIT_N + MAIN] = dot(gmat[0], part).astype(BF)
            tail = sum(dot(gmat[1 + k], part[:, k * w:(k + 1) * w]) for k in range(third))
            x_v[:, n * UNIT_N + MAIN:(n + 1) * UNIT_N] = tail.astype(BF)

    for n in range(n_out):
        base = n * k_out
        for k in range(k_out):
            out_unit(n, k, (base + k) % UNITS).wait()
        if n > 0:
            ship(n - 1)
        with jax.named_scope(f"out{n}"):
            done = []
            for s in range(UNIT_N // 256):
                cols = slice(n * UNIT_N + s * 256, n * UNIT_N + (s + 1) * 256)
                acc = None
                for k in range(k_out):
                    d = dot(h_v[:, k * UNIT_K:(k + 1) * UNIT_K], ring[(base + k) % UNITS, :, s * 256:(s + 1) * 256])
                    acc = d if acc is None else acc + d
                delta = (scale * dot(low_v[0], bdv[:, cols])).astype(BF).astype(F32)
                done.append((xc[:, cols].astype(F32) + (acc + delta)).astype(BF))
            done = jnp.concatenate(done, axis=1)
            both = dot(e_main, done[:, :MAIN]) + jnp.concatenate([dot(e, done[:, MAIN:]) for e in e_tail], axis=1)
            sent2(n)[...] = both.reshape(groups, slab, MAIN).astype(BF)
            recv2[n, 0] = sent2(n)[0]
        ahead = n + UNITS // k_out
        for k in range(k_out):
            if ahead < n_out:
                out_unit(ahead, k, (base + k) % UNITS).start()
        if n > 2:
            home(n - 3)
    ship(n_out - 1)
    for n in range(n_out - 3, n_out):
        home(n)
    last = in_copy(x_v, out_hbm, 7)
    last.start()
    last.wait()


def solution(mesh):
    groups = mesh.shape["data"]
    row_spec = P(("rep", "data"), None)
    id_spec = P(("rep", "data"))
    owned_spec = P("data", None, None)

    def device_step(x, adapter_id, w_gate, w_up, w_down, a_gate, b_gate, a_up, b_up, a_down, b_down):
        tok, dim = x.shape
        ff = w_gate.shape[1]
        per_owner, rank, _ = a_gate.shape
        stack = per_owner * rank
        cap = (3 * tok + groups - 1) // groups
        slots = groups * cap
        slab = 8
        n_out = dim // UNIT_N
        k_in = dim // UNIT_K
        width = UNIT_K // UNIT_N * MAIN
        flat = [m.reshape(stack, m.shape[2]) for m in (a_gate, b_gate, a_up, b_up, a_down, b_down)]
        anyspec = pl.BlockSpec(memory_space=pl.ANY)
        dma = pltpu.SemaphoreType.DMA
        return pl.pallas_call(
            functools.partial(layer, groups, cap, LORA_ALPHA / rank, rank),
            out_shape=jax.ShapeDtypeStruct((tok, dim), BF),
            in_specs=[pl.BlockSpec(memory_space=pltpu.VMEM)] + [anyspec] * 10,
            out_specs=anyspec,
            scratch_shapes=[
                pltpu.VMEM((UNITS, UNIT_K, UNIT_N), BF),
                pltpu.VMEM((2, slots, ff), F32),
                pltpu.VMEM((tok, dim), BF),
                pltpu.VMEM((slots, dim), BF),
                pltpu.VMEM((slots, ff), BF),
                pltpu.VMEM((2, stack, ff), BF),
                pltpu.VMEM((stack, ff), BF),
                pltpu.VMEM((stack, dim), BF),
                pltpu.VMEM((groups, slab, width + stack), BF),
                pltpu.VMEM((groups, slab, width + stack), BF),
                pltpu.VMEM((k_in - 1, groups, slab, width), BF),
                pltpu.VMEM((k_in - 1, groups, slab, width), BF),
                pltpu.VMEM((n_out, groups, slab, MAIN), BF),
                pltpu.VMEM((slots, stack), F32),
                pltpu.VMEM((2, slots, stack), BF),
                pltpu.VMEM((1 + cap // 2, tok, groups * slab), BF),
                dma((UNITS,)), dma((8,)), dma((k_in, groups)), dma((k_in, groups)), dma((n_out, groups)), dma((n_out, groups)),
            ],
            compiler_params=pltpu.CompilerParams(collective_id=0, has_side_effects=True, vmem_limit_bytes=67043328),
            name="lora_swiglu",
        )(adapter_id.reshape(1, tok), x, w_gate, w_up, w_down, *flat)

    return jax.shard_map(device_step, mesh=mesh, in_specs=(row_spec, id_spec, P(), P(), P(), owned_spec, owned_spec, owned_spec, owned_spec, owned_spec, owned_spec), out_specs=row_spec, check_vma=False)
```

time: 158 us -> 81.5 us (0.52)
  matrix products: 89.4 us -> 0 us
  Pallas kernels: 0 us -> 79.6 us
  blocking collectives: 60.2 us -> 0 us
  local copies, waits for them, and re-layouts: 6.74 us -> 1.77 us
    dot_general x8 -> x0, matrix products: 89.4 us -> none  [the longest x1 24.7 us: device_step(): jnp.dot(xr, w_up, preferred_element_type=jnp.float32)]
    pallas_call x0 -> x1, Pallas kernels: none -> 79.6 us  [device_step(): pl.pallas_call(functools.partial(layer, groups, cap, LORA_ALPHA / rank, r...]
    all_to_all x2 -> x0, blocking collectives: 60.2 us -> none  [the longest x1 33.2 us: device_step(): recv = lax.all_to_all(send, 'data', 0, 0, tiled=True)]
    all_to_all x4 -> x0, local copies, waits for them, and re-layouts: 6.73 us -> none  [the longest x2 3.78 us: device_step(): recv = lax.all_to_all(send, 'data', 0, 0, tiled=True)]
    unnamed x8 -> x1, local copies, waits for them, and re-layouts: 0.02 us -> 1.77 us
where the time goes in v2:
time: 81.5 us; the launch traced here: 81.4 us
  Pallas kernels  79.6 us (98%)
  local copies, waits for them, and re-layouts  1.77 us (2%)
    pallas_call x1, Pallas kernels, device_step(): pl.pallas_call(functools.partial(layer, groups, cap, LORA_ALPHA / rank, r...  79.6 us
    unnamed x1, local copies, waits for them, and re-layouts  1.77 us

profile of v2, /device:TPU:97, one launch (start us, length us, event | category | flops | bytes accessed | tf_op | source)
XLA Modules:
  0.0 81.4 jit_solution(11999366160506748688)
XLA Ops:
  0.0 79.6 %lora_swiglu.1 = bf16[64,3072]{1,0:T(8,128)(2,1)} custom-call(s32[1,64]{1,0:T(1,128)} %bitcast.13, bf16[64,3072]{1,0:T(8,128)(2,1)} %x_hbm.1, bf16[3072,8192]{1,0:T(8,128)(2,1)} %wg_hbm.1, bf16[3072,8192]{1,0:T(8,128)(2,1)} %wu_hbm.1, bf16[8192,3072]{1,0:T(8,128)(2,1)} %wd_hbm.1, bf16[128,3072]{1,0:T(8,128)(2,1)} %bitcast.10, bf16[128,8192]{1,0:T(8,128)(2,1)} %bitcast.7, ...), custom_call_target="tpu_custom_call" | custom-call | tf_op jit(solution)/shard_map/lora_swiglu/pallas_call | solution.py:340
  79.6 1.8 %copy.13 = bf16[64,3072]{1,0:T(8,128)(2,1)} copy(bf16[64,3072]{1,0:T(8,128)(2,1)} %lora_swiglu.1) | data formatting | bytes 786432

commit v3 on v2

v3 whole, which is shorter than its diff:
```python
import functools
import math

import jax
import jax.numpy as jnp
from jax import lax
from jax.experimental import pallas as pl
from jax.experimental.pallas import tpu as pltpu
from jax.sharding import PartitionSpec as P

LORA_ALPHA = 32
BF, F32 = jnp.bfloat16, jnp.float32
CORES = 2
UNIT_K, UNIT_N = 1024, 512
UNITS = 32
MAIN = 384


def one_hot(rows, cols, hit):
    r = lax.broadcasted_iota(jnp.int32, (rows, cols), 0)
    c = lax.broadcasted_iota(jnp.int32, (rows, cols), 1)
    return hit(r, c).astype(F32).astype(BF)


def dot(a, b):
    return jnp.dot(a, b, preferred_element_type=F32)


def dot_t(a, b):
    return lax.dot_general(a, b, (((1,), (1,)), ((), ())), preferred_element_type=F32)


def layer(groups, cap, scale, rank, ids_ref, x_hbm, wg_hbm, wu_hbm, wd_hbm, ag_hbm, bg_hbm, au_hbm, bu_hbm, ad_hbm, bd_hbm, out_hbm,
          ring, acc_v, x_v, xc, h_v, bgu, adv, bdv, sendx, recvx, sendm, recvm, land, keep_v, low_v, gmat, unmap, remap,
          ring_sem, in_sem, s1_sem, r1_sem, s2_sem, land_sem):
    tok, dim = x_v.shape
    ff = h_v.shape[1]
    stack = bdv.shape[0]
    slots = groups * cap
    slab = recvm.shape[2]
    packed = groups * slab
    side = math.isqrt(groups // CORES)
    third = cap // 2
    n_in = ff // UNIT_N
    n_out = dim // UNIT_N
    k_out = ff // UNIT_K
    passes = ((0, 1), (1, 1)) + tuple((c, 2) for c in range(2, n_out, 2))
    last_pass = len(passes) - 1
    me = lax.axis_index("data")
    my_c, my_x, my_y = lax.rem(me, CORES), lax.rem(me // CORES, side), me // (CORES * side)

    chips = side * side

    def device(dy, dx, dc):
        return {"data": (lax.rem(my_y + dy % side, side) * side + lax.rem(my_x + dx % side, side)) * CORES + lax.rem(my_c + dc, CORES)}

    def target(r, back=False):
        sign = -1 if back else 1
        return device(sign * (r // (CORES * side)), sign * ((r // CORES) % side), r % CORES)

    def hops(r):
        dy, dx = r // (CORES * side), (r // CORES) % side
        return min(dy, side - dy) + min(dx, side - dx)

    order = sorted(range(1, groups), key=lambda r: -hops(r))

    def remote(src, dst, ssem, rsem, to):
        return pltpu.make_async_remote_copy(src, dst, ssem, rsem, device_id=to, device_id_type=pl.DeviceIdType.MESH)

    per_step = 8

    def in_copy(src, dst, i):
        return pltpu.make_async_copy(src, dst, in_sem.at[i])

    def fill(p, base, unit, slot):
        c, n = passes[p]
        rows = n * UNIT_N
        per = 2 // n
        for part in range(per):
            which = part if per == 2 else unit % 2
            block = (base + unit) if per == 2 else base // 2 + unit // 2
            col = pl.multiple_of(block * UNIT_N, UNIT_N)
            src = (wg_hbm, wu_hbm)[which].at[pl.ds(c * UNIT_N, rows), pl.ds(col, UNIT_N)]
            pltpu.make_async_copy(src, ring.at[slot, pl.ds(part * rows, rows)], ring_sem.at[lax.div(slot, per_step)]).start()

    def filled(slot):
        ref = ring.at[pl.ds(slot, per_step)]
        pltpu.make_async_copy(ref, ref, ring_sem.at[lax.div(slot, per_step)]).wait()

    def out_unit(n, k, slot):
        col = pl.multiple_of(n * UNIT_N, UNIT_N)
        return pltpu.make_async_copy(wd_hbm.at[pl.ds(k * UNIT_K, UNIT_K), pl.ds(col, UNIT_N)], ring.at[slot], ring_sem.at[lax.div(slot, per_step)])

    x_copy = in_copy(x_hbm, x_v, 0)
    x_copy.start()
    early = [in_copy(ag_hbm, h_v.at[pl.ds(0, stack), pl.ds(0, dim)], 1), in_copy(au_hbm, h_v.at[pl.ds(0, stack), pl.ds(dim, dim)], 2),
             in_copy(bg_hbm, bgu.at[0], 3), in_copy(bu_hbm, bgu.at[1], 4)]
    late = [in_copy(ad_hbm, adv, 5), in_copy(bd_hbm, bdv, 6)]

    with jax.named_scope("signal"):
        barrier = pltpu.get_barrier_semaphore()
        for r in range(1, groups):
            pl.semaphore_signal(barrier, inc=1, device_id=target(r), device_id_type=pl.DeviceIdType.MESH)

    with jax.named_scope("place"):
        ids = ids_ref[...].astype(F32)
        eye = lax.broadcasted_iota(jnp.int32, (tok, tok), 0) == lax.broadcasted_iota(jnp.int32, (tok, tok), 1)
        ids_c = jnp.sum(jnp.where(eye, jnp.broadcast_to(ids, (tok, tok)), 0.0), axis=1, keepdims=True)
        per_owner = stack // rank

        def fdiv(v, n):
            return jnp.floor((v + 0.5) * (1.0 / n))

        def place(v):
            owner = fdiv(v, per_owner)
            local = v - owner * per_owner
            oy = fdiv(owner, CORES * side)
            ox = fdiv(owner, CORES) - oy * side
            oc = owner - fdiv(owner, CORES) * CORES

            def mod(a, b, n):
                d = a - b.astype(F32)
                return jnp.where(d < 0, d + n, d)
            rel = (mod(oy, my_y, side) * side + mod(ox, my_x, side)) * CORES + mod(oc, my_c, CORES)
            return owner, local, rel

        own_r, _, rel_r = place(ids)
        own_c, loc_c, rel_c = place(ids_c)
        t0 = lax.broadcasted_iota(jnp.int32, (tok, tok), 0)
        t1 = lax.broadcasted_iota(jnp.int32, (tok, tok), 1)
        same = own_c == own_r
        arr_r = jnp.sum(jnp.where(same & (t0 < t1), 1.0, 0.0), axis=0, keepdims=True)
        arr_c = jnp.sum(jnp.where(same & (t1 < t0), 1.0, 0.0), axis=1, keepdims=True)

        def rows_of(rel, arr):
            main = (rel * slab + arr).astype(jnp.int32)
            tail_row = fdiv(arr, third)
            tail = (rel * slab + cap + tail_row).astype(jnp.int32)
            part = (arr - tail_row * third).astype(jnp.int32)
            return main, tail, part

        main_r, tail_r, part_r = rows_of(rel_r, arr_r)
        main_c, tail_c, part_c = rows_of(rel_c, arr_c)
        s_main = one_hot(packed, tok, lambda r, c: r == main_r)
        s_tail = [one_hot(packed, tok, lambda r, c: (r == tail_r) & (part_r == k)) for k in range(third)]
        gmat[0] = one_hot(tok, packed, lambda r, c: c == main_c)
        for k in range(third):
            gmat[1 + k] = one_hot(tok, packed, lambda r, c: (c == tail_c) & (part_c == k))
        mine = one_hot(tok, stack, lambda r, c: loc_c == fdiv(c.astype(F32), rank))

    with jax.named_scope("x_wait"):
        x_copy.wait()
    with jax.named_scope("weights"):
        for p in range(2):
            for u in range(UNITS // 2):
                fill(p, 0, u, p * (UNITS // 2) + u)
        for c in early + late:
            c.start()

    n_pass = len(passes)

    def copy1(p, r):
        q, dc = r // CORES, r % CORES
        if p == n_pass:
            src, dst = sendm.at[q, dc], recvm.at[q, dc]
        else:
            at = pl.ds(*passes[p])
            src, dst = sendx.at[at, q, dc], recvx.at[at, q, dc]
        near = int(q == 0)
        return remote(src, dst, s1_sem.at[int(p == n_pass), near], r1_sem.at[p, near], target(r))

    others = pl.ds(1, chips - 1)

    def all_of(ref, ssem, rsem):
        return remote(ref, ref, ssem, rsem, target(1))

    for p in range(n_pass + 1):
        with jax.named_scope(f"pack{p}"):
            if p == n_pass:
                sendm[...] = dot(s_main, mine).reshape(chips, CORES, slab, stack).astype(BF)
            else:
                for b in range(passes[p][0], sum(passes[p])):
                    xa = x_v[:, b * UNIT_N:b * UNIT_N + MAIN]
                    xb = x_v[:, b * UNIT_N + MAIN:(b + 1) * UNIT_N]
                    both = dot(s_main, xa) + jnp.concatenate([dot(s, xb) for s in s_tail], axis=1)
                    sendx[b] = both.reshape(chips, CORES, slab, MAIN).astype(BF)
        if p == 0:
            with jax.named_scope("bar_wait"):
                pl.semaphore_wait(barrier, groups - 1)
        with jax.named_scope(f"send{p}"):
            for r in order:
                copy1(p, r).start()
            if p == n_pass:
                recvm[0, 0] = sendm[0, 0]
            else:
                for b in range(passes[p][0], sum(passes[p])):
                    recvx[b, 0, 0] = sendx[b, 0, 0]

    def slot_of(s):
        g = fdiv(s.astype(F32), cap).astype(jnp.int32)
        return g, s - g * cap

    def unpack_main(r, c):
        g, j = slot_of(r)
        return c == g * slab + j

    def unpack_tail(k):
        def hit(r, c):
            g, j = slot_of(r)
            q = fdiv(j.astype(F32), third).astype(jnp.int32)
            return (c == g * slab + cap + q) & (j - q * third == k)
        return hit

    def pack_main(r, c):
        return unpack_main(c, r)

    def pack_tail(k):
        def hit(r, c):
            return unpack_tail(k)(c, r)
        return hit

    with jax.named_scope("maps"):
        unmap[0] = one_hot(slots, packed, unpack_main)
        remap[0] = one_hot(packed, slots, pack_main)
        for k in range(third):
            unmap[1 + k] = one_hot(slots, packed, unpack_tail(k))
            remap[1 + k] = one_hot(packed, slots, pack_tail(k))
    w = MAIN // third

    def dense(v):
        return v.astype(F32).reshape(packed, v.shape[-1]).astype(BF)

    def arrive(p):
        with jax.named_scope(f"recv{p}"):
            if p == n_pass:
                all_of(recvm.at[others], s1_sem.at[1, 0], r1_sem.at[p, 0]).wait_recv()
                all_of(recvm.at[0, 1], s1_sem.at[1, 1], r1_sem.at[p, 1]).wait_recv()
            else:
                at = pl.ds(*passes[p])
                all_of(recvx.at[at, others], s1_sem.at[0, 0], r1_sem.at[p, 0]).wait_recv()
                all_of(recvx.at[at, 0, 1], s1_sem.at[0, 1], r1_sem.at[p, 1]).wait_recv()
        with jax.named_scope(f"unpack{p}"):
            if p == n_pass:
                keep_v[...] = dot(unmap[0], dense(recvm[...]))
            else:
                for b in range(passes[p][0], sum(passes[p])):
                    part = dense(recvx[b])
                    xc[:, b * UNIT_N:b * UNIT_N + MAIN] = dot(unmap[0], part).astype(BF)
                    tail = sum(dot(unmap[1 + k], part[:, k * w:(k + 1) * w]) for k in range(third))
                    xc[:, b * UNIT_N + MAIN:(b + 1) * UNIT_N] = tail.astype(BF)

    def pick(low):
        return jnp.where(keep_v[...] > 0.5, low.astype(BF).astype(F32), 0.0).astype(BF)

    for p in range(n_pass):
        arrive(p)
        c, n = passes[p]
        rows = n * UNIT_N
        if p == last_pass:
            arrive(n_pass)
            with jax.named_scope("low"):
                for cp in early:
                    cp.wait()
                for i in range(2):
                    low_v[i] = pick(sum(dot_t(xc[:, k:k + UNIT_N], h_v[0:stack, i * dim + k:i * dim + k + UNIT_N]) for k in range(0, dim, UNIT_N)))
        start = p * (UNITS // 2) if n == 1 else 0
        blocks = per_step if n == 1 else per_step // 2

        def step(i, carry):
            base = i * per_step
            filled(pl.multiple_of(start + base, per_step))
            with jax.named_scope(f"dot{p}"):
                for b in range(blocks):
                    for s in range(UNIT_N // 256):
                        col = pl.ds(pl.multiple_of((i * blocks + b) * UNIT_N + s * 256, 256), 256)
                        res = []
                        for which in range(2):
                            slot, row = (start + base + b, which * rows) if n == 1 else (base + b * 2 + which, 0)
                            d = dot(xc[:, c * UNIT_N:c * UNIT_N + rows], ring[slot, row:row + rows, s * 256:(s + 1) * 256])
                            if p > 0:
                                d = acc_v[which, :, col] + d
                            if p < last_pass:
                                acc_v[which, :, col] = d
                            else:
                                res.append(d + (scale * dot(low_v[which], bgu[which, :, col])).astype(BF).astype(F32))
                        if res:
                            g, u = res
                            h_v[:, col] = (g * (1.0 / (1.0 + jnp.exp(-g))) * u).astype(BF)
            for k in range(per_step):
                slot = start + base + k
                if p == last_pass:
                    out_unit(i, k, slot).start()
                elif p == 0:
                    fill(2, base, k, slot)
                elif p == 1:
                    fill(2, base + UNITS // 2, k, slot)
                else:
                    fill(p + 1, base, k, slot)
            return carry

        lax.fori_loop(0, (UNITS // 2 if n == 1 else UNITS) // per_step, step, 0)

    with jax.named_scope("low2"):
        for cp in late:
            cp.wait()
        @pl.when(me >= 0)
        def _():
            low_v[0] = pick(sum(dot_t(h_v[:, k:k + UNIT_K], adv[:, k:k + UNIT_K]) for k in range(0, ff, UNIT_K)))
    all_of(sendx.at[:, others], s1_sem.at[0, 0], r1_sem.at[0, 0]).wait_send()
    all_of(sendx.at[:, 0, 1], s1_sem.at[0, 1], r1_sem.at[0, 1]).wait_send()
    all_of(sendm.at[others], s1_sem.at[1, 0], r1_sem.at[0, 0]).wait_send()
    all_of(sendm.at[0, 1], s1_sem.at[1, 1], r1_sem.at[0, 1]).wait_send()

    def ship(n):
        with jax.named_scope(f"ship{n}"):
            for r in order:
                q, dc = r // CORES, r % CORES
                near = int(q == 0)
                remote(sendx.at[n, q, dc], land.at[n, q, dc], s2_sem.at[near], land_sem.at[n, near], target(r, True)).start()

    def home(n):
        with jax.named_scope(f"homewait{n}"):
            all_of(land.at[n, others], s2_sem.at[0], land_sem.at[n, 0]).wait_recv()
            all_of(land.at[n, 0, 1], s2_sem.at[1], land_sem.at[n, 1]).wait_recv()
        with jax.named_scope(f"home{n}"):
            part = dense(land[n])
            x_v[:, n * UNIT_N:n * UNIT_N + MAIN] = dot(gmat[0], part).astype(BF)
            tail = sum(dot(gmat[1 + k], part[:, k * w:(k + 1) * w]) for k in range(third))
            x_v[:, n * UNIT_N + MAIN:(n + 1) * UNIT_N] = tail.astype(BF)

    for n in range(n_out):
        base = n * k_out
        filled(base % UNITS)
        if n > 0:
            ship(n - 1)
        with jax.named_scope(f"out{n}"):
            done = []
            for s in range(UNIT_N // 256):
                cols = slice(n * UNIT_N + s * 256, n * UNIT_N + (s + 1) * 256)
                acc = None
                for k in range(k_out):
                    d = dot(h_v[:, k * UNIT_K:(k + 1) * UNIT_K], ring[(base + k) % UNITS, :, s * 256:(s + 1) * 256])
                    acc = d if acc is None else acc + d
                delta = (scale * dot(low_v[0], bdv[:, cols])).astype(BF).astype(F32)
                done.append((xc[:, cols].astype(F32) + (acc + delta)).astype(BF))
            done = jnp.concatenate(done, axis=1)
            both = dot(remap[0], done[:, :MAIN]) + jnp.concatenate([dot(remap[1 + k], done[:, MAIN:]) for k in range(third)], axis=1)
            sendx[n] = both.reshape(chips, CORES, slab, MAIN).astype(BF)
            land[n, 0, 0] = sendx[n, 0, 0]
        ahead = n + UNITS // k_out
        for k in range(k_out):
            if ahead < n_out:
                out_unit(ahead, k, (base + k) % UNITS).start()
        if n > 2:
            home(n - 3)
    ship(n_out - 1)
    for n in range(n_out - 3, n_out):
        home(n)
    all_of(sendx.at[:, others], s2_sem.at[0], land_sem.at[0, 0]).wait_send()
    all_of(sendx.at[:, 0, 1], s2_sem.at[1], land_sem.at[0, 1]).wait_send()
    last = in_copy(x_v, out_hbm, 7)
    last.start()
    last.wait()


def solution(mesh):
    groups = mesh.shape["data"]
    row_spec = P(("rep", "data"), None)
    id_spec = P(("rep", "data"))
    owned_spec = P("data", None, None)

    def device_step(x, adapter_id, w_gate, w_up, w_down, a_gate, b_gate, a_up, b_up, a_down, b_down):
        tok, dim = x.shape
        ff = w_gate.shape[1]
        per_owner, rank, _ = a_gate.shape
        stack = per_owner * rank
        cap = (3 * tok + groups - 1) // groups
        slots = groups * cap
        slab = 8
        n_out = dim // UNIT_N
        chips = groups // CORES
        flat = [m.reshape(stack, m.shape[2]) for m in (a_gate, b_gate, a_up, b_up, a_down, b_down)]
        anyspec = pl.BlockSpec(memory_space=pl.ANY)
        dma = pltpu.SemaphoreType.DMA
        return pl.pallas_call(
            functools.partial(layer, groups, cap, LORA_ALPHA / rank, rank),
            out_shape=jax.ShapeDtypeStruct((tok, dim), BF),
            in_specs=[pl.BlockSpec(memory_space=pltpu.VMEM)] + [anyspec] * 10,
            out_specs=anyspec,
            scratch_shapes=[
                pltpu.VMEM((UNITS, UNIT_K, UNIT_N), BF),
                pltpu.VMEM((2, slots, ff), F32),
                pltpu.VMEM((tok, dim), BF),
                pltpu.VMEM((slots, dim), BF),
                pltpu.VMEM((slots, ff), BF),
                pltpu.VMEM((2, stack, ff), BF),
                pltpu.VMEM((stack, ff), BF),
                pltpu.VMEM((stack, dim), BF),
                pltpu.VMEM((n_out, chips, CORES, slab, MAIN), BF),
                pltpu.VMEM((n_out, chips, CORES, slab, MAIN), BF),
                pltpu.VMEM((chips, CORES, slab, stack), BF),
                pltpu.VMEM((chips, CORES, slab, stack), BF),
                pltpu.VMEM((n_out, chips, CORES, slab, MAIN), BF),
                pltpu.VMEM((slots, stack), F32),
                pltpu.VMEM((2, slots, stack), BF),
                pltpu.VMEM((1 + cap // 2, tok, groups * slab), BF),
                pltpu.VMEM((1 + cap // 2, slots, groups * slab), BF),
                pltpu.VMEM((1 + cap // 2, groups * slab, slots), BF),
                dma((UNITS // 8,)), dma((8,)), dma((2, 2)), dma((n_out, 2)), dma((2,)), dma((n_out, 2)),
            ],
            compiler_params=pltpu.CompilerParams(collective_id=0, has_side_effects=True, vmem_limit_bytes=67043328),
            name="lora_swiglu",
        )(adapter_id.reshape(1, tok), x, w_gate, w_up, w_down, *flat)

    return jax.shard_map(device_step, mesh=mesh, in_specs=(row_spec, id_spec, P(), P(), P(), owned_spec, owned_spec, owned_spec, owned_spec, owned_spec, owned_spec), out_specs=row_spec, check_vma=False)
```

time: 81.5 us -> 70.1 us (0.86)
  Pallas kernels: 79.6 us -> 68.2 us
    pallas_call x1, Pallas kernels: 79.6 us -> 68.2 us  [device_step(): pl.pallas_call(functools.partial(layer, groups, cap, LORA_ALPHA / rank, r...]
where the time goes in v3:
time: 70.1 us; the launch traced here: 70 us
  Pallas kernels  68.2 us (97%)
  local copies, waits for them, and re-layouts  1.77 us (3%)
    pallas_call x1, Pallas kernels, device_step(): pl.pallas_call(functools.partial(layer, groups, cap, LORA_ALPHA / rank, r...  68.2 us
    unnamed x1, local copies, waits for them, and re-layouts  1.77 us

profile of v3, /device:TPU:97, one launch (start us, length us, event | category | flops | bytes accessed | tf_op | source)
XLA Modules:
  0.0 70.0 jit_solution(11714114971177596341)
XLA Ops:
  0.0 68.2 %lora_swiglu.1 = bf16[64,3072]{1,0:T(8,128)(2,1)} custom-call(s32[1,64]{1,0:T(1,128)} %bitcast.13, bf16[64,3072]{1,0:T(8,128)(2,1)} %x_hbm.1, bf16[3072,8192]{1,0:T(8,128)(2,1)} %wg_hbm.1, bf16[3072,8192]{1,0:T(8,128)(2,1)} %wu_hbm.1, bf16[8192,3072]{1,0:T(8,128)(2,1)} %wd_hbm.1, bf16[128,3072]{1,0:T(8,128)(2,1)} %bitcast.10, bf16[128,8192]{1,0:T(8,128)(2,1)} %bitcast.7, ...), custom_call_target="tpu_custom_call" | custom-call | tf_op jit(solution)/shard_map/lora_swiglu/pallas_call | solution.py:385
  68.2 1.8 %copy.13 = bf16[64,3072]{1,0:T(8,128)(2,1)} copy(bf16[64,3072]{1,0:T(8,128)(2,1)} %lora_swiglu.1) | data formatting | bytes 786432

commit v4 on v3

--- a/solution.py
+++ b/solution.py
@@ -13,6 +13,7 @@
 CORES = 2
 UNIT_K, UNIT_N = 1024, 512
 UNITS = 32
+GROUPS = 2
 MAIN = 384
 
 
@@ -30,9 +31,9 @@
     return lax.dot_general(a, b, (((1,), (1,)), ((), ())), preferred_element_type=F32)
 
 
-def layer(groups, cap, scale, rank, ids_ref, x_hbm, wg_hbm, wu_hbm, wd_hbm, ag_hbm, bg_hbm, au_hbm, bu_hbm, ad_hbm, bd_hbm, out_hbm,
+def layer(groups, cap, scale, rank, ids_ref, x_hbm, wg_hbm, wu_hbm, wd_hbm, ag_hbm, bg_hbm, au_hbm, bu_hbm, ad_hbm, bd_hbm, out_v,
           ring, acc_v, x_v, xc, h_v, bgu, adv, bdv, sendx, recvx, sendm, recvm, land, keep_v, low_v, gmat, unmap, remap,
-          ring_sem, in_sem, s1_sem, r1_sem, s2_sem, land_sem):
+          ring_sem, in_sem, s1_sem, r1_sem, s2_sem, land_sem, part_sem, free_sem):
     tok, dim = x_v.shape
     ff = h_v.shape[1]
     stack = bdv.shape[0]
@@ -93,14 +94,14 @@
 
     x_copy = in_copy(x_hbm, x_v, 0)
     x_copy.start()
+    with jax.named_scope("signal"):
+        barrier = pltpu.get_barrier_semaphore()
+        for r in order:
+            pl.semaphore_signal(barrier, inc=1, device_id=target(r), device_id_type=pl.DeviceIdType.MESH)
+
     early = [in_copy(ag_hbm, h_v.at[pl.ds(0, stack), pl.ds(0, dim)], 1), in_copy(au_hbm, h_v.at[pl.ds(0, stack), pl.ds(dim, dim)], 2),
              in_copy(bg_hbm, bgu.at[0], 3), in_copy(bu_hbm, bgu.at[1], 4)]
     late = [in_copy(ad_hbm, adv, 5), in_copy(bd_hbm, bdv, 6)]
-
-    with jax.named_scope("signal"):
-        barrier = pltpu.get_barrier_semaphore()
-        for r in range(1, groups):
-            pl.semaphore_signal(barrier, inc=1, device_id=target(r), device_id_type=pl.DeviceIdType.MESH)
 
     with jax.named_scope("place"):
         ids = ids_ref[...].astype(F32)
@@ -154,8 +155,6 @@
         for p in range(2):
             for u in range(UNITS // 2):
                 fill(p, 0, u, p * (UNITS // 2) + u)
-        for c in early + late:
-            c.start()
 
     n_pass = len(passes)
 
@@ -258,19 +257,25 @@
         rows = n * UNIT_N
         if p == last_pass:
             arrive(n_pass)
+            pl.semaphore_signal(free_sem, inc=1, device_id=device(0, 0, 1), device_id_type=pl.DeviceIdType.MESH)
             with jax.named_scope("low"):
                 for cp in early:
                     cp.wait()
                 for i in range(2):
                     low_v[i] = pick(sum(dot_t(xc[:, k:k + UNIT_N], h_v[0:stack, i * dim + k:i * dim + k + UNIT_N]) for k in range(0, dim, UNIT_N)))
         start = p * (UNITS // 2) if n == 1 else 0
-        blocks = per_step if n == 1 else per_step // 2
+        size = (GROUPS if n == 1 else 1) * per_step
+        blocks = size if n == 1 else size // 2
 
         def step(i, carry):
-            base = i * per_step
-            filled(pl.multiple_of(start + base, per_step))
+            base = i * size
+            if n == 1:
+                for g in range(GROUPS):
+                    filled(start + base + g * per_step)
             with jax.named_scope(f"dot{p}"):
                 for b in range(blocks):
+                    if n > 1 and b * size // blocks % per_step == 0:
+                        filled(start + base + b * size // blocks)
                     for s in range(UNIT_N // 256):
                         col = pl.ds(pl.multiple_of((i * blocks + b) * UNIT_N + s * 256, 256), 256)
                         res = []
@@ -286,19 +291,31 @@
                         if res:
                             g, u = res
                             h_v[:, col] = (g * (1.0 / (1.0 + jnp.exp(-g))) * u).astype(BF)
-            for k in range(per_step):
-                slot = start + base + k
-                if p == last_pass:
-                    out_unit(i, k, slot).start()
-                elif p == 0:
-                    fill(2, base, k, slot)
-                elif p == 1:
-                    fill(2, base + UNITS // 2, k, slot)
-                else:
-                    fill(p + 1, base, k, slot)
+                    if (b + 1) * size // blocks % per_step:
+                        continue
+                    for k in range((b + 1) * size // blocks - per_step, (b + 1) * size // blocks):
+                        slot = start + base + k
+                        if p == last_pass:
+                            out_unit(i * size // per_step + k // per_step, k % per_step, slot).start()
+                        elif p == 0:
+                            fill(2, base, k, slot)
+                        elif p == 1:
+                            fill(2, base + UNITS // 2, k, slot)
+                        else:
+                            fill(p + 1, base, k, slot)
             return carry
 
-        lax.fori_loop(0, (UNITS // 2 if n == 1 else UNITS) // per_step, step, 0)
+        steps = (UNITS // 2 if n == 1 else UNITS) // size
+        if p == last_pass:
+            for cp in late:
+                cp.start()
+        if steps == 1:
+            step(0, 0)
+        else:
+            lax.fori_loop(0, steps, step, 0)
+        if p == 1:
+            for cp in early:
+                cp.start()
 
     with jax.named_scope("low2"):
         for cp in late:
@@ -318,21 +335,42 @@
                 near = int(q == 0)
                 remote(sendx.at[n, q, dc], land.at[n, q, dc], s2_sem.at[near], land_sem.at[n, near], target(r, True)).start()
 
+    chip_order = [r // CORES for r in order if r % CORES == 0]
+
+    def ship_pairs(n):
+        with jax.named_scope(f"shipp{n}"):
+            for q in chip_order:
+                remote(sendx.at[n, q], land.at[n, q], s2_sem.at[2], land_sem.at[n, 0], target(q * CORES, True)).start()
+
+    def hand_on(n):
+        with jax.named_scope(f"hand{n}"):
+            all_of(land.at[n, others], s2_sem.at[2], land_sem.at[n, 0]).wait_recv()
+            if n == 0:
+                pl.semaphore_wait(free_sem, 1)
+            remote(land.at[n, :, 1], recvx.at[n, :, 1], s2_sem.at[3], part_sem.at[n], device(0, 0, 1)).start()
+
     def home(n):
         with jax.named_scope(f"homewait{n}"):
-            all_of(land.at[n, others], s2_sem.at[0], land_sem.at[n, 0]).wait_recv()
-            all_of(land.at[n, 0, 1], s2_sem.at[1], land_sem.at[n, 1]).wait_recv()
+            if n < n_out - 1:
+                all_of(recvx.at[n, :, 1], s2_sem.at[3], part_sem.at[n]).wait_recv()
+                slabs = jnp.concatenate([land[n, :, 0:1], recvx[n, :, 1:2]], axis=1)
+            else:
+                all_of(land.at[n, others], s2_sem.at[0], land_sem.at[n, 0]).wait_recv()
+                all_of(land.at[n, 0, 1], s2_sem.at[1], land_sem.at[n, 1]).wait_recv()
+                slabs = land[n]
         with jax.named_scope(f"home{n}"):
-            part = dense(land[n])
-            x_v[:, n * UNIT_N:n * UNIT_N + MAIN] = dot(gmat[0], part).astype(BF)
+            part = dense(slabs)
+            out_v[:, n * UNIT_N:n * UNIT_N + MAIN] = dot(gmat[0], part).astype(BF)
             tail = sum(dot(gmat[1 + k], part[:, k * w:(k + 1) * w]) for k in range(third))
-            x_v[:, n * UNIT_N + MAIN:(n + 1) * UNIT_N] = tail.astype(BF)
+            out_v[:, n * UNIT_N + MAIN:(n + 1) * UNIT_N] = tail.astype(BF)
 
     for n in range(n_out):
         base = n * k_out
         filled(base % UNITS)
         if n > 0:
-            ship(n - 1)
+            ship_pairs(n - 1)
+        if n > 3:
+            hand_on(n - 4)
         with jax.named_scope(f"out{n}"):
             done = []
             for s in range(UNIT_N // 256):
@@ -346,21 +384,24 @@
             done = jnp.concatenate(done, axis=1)
             both = dot(remap[0], done[:, :MAIN]) + jnp.concatenate([dot(remap[1 + k], done[:, MAIN:]) for k in range(third)], axis=1)
             sendx[n] = both.reshape(chips, CORES, slab, MAIN).astype(BF)
-            land[n, 0, 0] = sendx[n, 0, 0]
+            if n < n_out - 1:
+                land[n, 0] = sendx[n, 0]
+            else:
+                land[n, 0, 0] = sendx[n, 0, 0]
         ahead = n + UNITS // k_out
         for k in range(k_out):
             if ahead < n_out:
                 out_unit(ahead, k, (base + k) % UNITS).start()
-        if n > 2:
-            home(n - 3)
-    ship(n_out - 1)
-    for n in range(n_out - 3, n_out):
+    m = n_out - 1
+    ship(m)
+    for n in range(m - 3, m):
+        hand_on(n)
+    for n in range(n_out):
         home(n)
-    all_of(sendx.at[:, others], s2_sem.at[0], land_sem.at[0, 0]).wait_send()
-    all_of(sendx.at[:, 0, 1], s2_sem.at[1], land_sem.at[0, 1]).wait_send()
-    last = in_copy(x_v, out_hbm, 7)
-    last.start()
-    last.wait()
+    all_of(sendx.at[m, others], s2_sem.at[0], land_sem.at[0, 0]).wait_send()
+    all_of(sendx.at[m, 0, 1], s2_sem.at[1], land_sem.at[0, 1]).wait_send()
+    all_of(sendx.at[pl.ds(0, m), others], s2_sem.at[2], land_sem.at[0, 0]).wait_send()
+    all_of(land.at[pl.ds(0, m), :, 1], s2_sem.at[3], part_sem.at[0]).wait_send()
 
 
 def solution(mesh):
@@ -386,7 +427,7 @@
             functools.partial(layer, groups, cap, LORA_ALPHA / rank, rank),
             out_shape=jax.ShapeDtypeStruct((tok, dim), BF),
             in_specs=[pl.BlockSpec(memory_space=pltpu.VMEM)] + [anyspec] * 10,
-            out_specs=anyspec,
+            out_specs=pl.BlockSpec(memory_space=pltpu.VMEM),
             scratch_shapes=[
                 pltpu.VMEM((UNITS, UNIT_K, UNIT_N), BF),
                 pltpu.VMEM((2, slots, ff), F32),
@@ -406,7 +447,7 @@
                 pltpu.VMEM((1 + cap // 2, tok, groups * slab), BF),
                 pltpu.VMEM((1 + cap // 2, slots, groups * slab), BF),
                 pltpu.VMEM((1 + cap // 2, groups * slab, slots), BF),
-                dma((UNITS // 8,)), dma((8,)), dma((2, 2)), dma((n_out, 2)), dma((2,)), dma((n_out, 2)),
+                dma((UNITS // 8,)), dma((8,)), dma((2, 2)), dma((n_out, 2)), dma((4,)), dma((n_out, 2)), dma((n_out - 1,)), pltpu.SemaphoreType.REGULAR,
             ],
             compiler_params=pltpu.CompilerParams(collective_id=0, has_side_effects=True, vmem_limit_bytes=67043328),
             name="lora_swiglu",

time: 70.1 us -> 66.4 us (0.947)
  Pallas kernels: 68.2 us -> 64.5 us
    pallas_call x1, Pallas kernels: 68.2 us -> 64.5 us  [device_step(): pl.pallas_call(functools.partial(layer, groups, cap, LORA_ALPHA / rank, r...]
where the time goes in v4:
time: 66.4 us; the launch traced here: 66.3 us
  Pallas kernels  64.5 us (97%)
  local copies, waits for them, and re-layouts  1.77 us (3%)
    pallas_call x1, Pallas kernels, device_step(): pl.pallas_call(functools.partial(layer, groups, cap, LORA_ALPHA / rank, r...  64.5 us
    unnamed x1, local copies, waits for them, and re-layouts  1.77 us

profile of v4, /device:TPU:97, one launch (start us, length us, event | category | flops | bytes accessed | tf_op | source)
XLA Modules:
  0.0 66.3 jit_solution(2616828158439244830)
XLA Ops:
  0.0 64.5 %lora_swiglu.1 = bf16[64,3072]{1,0:T(8,128)(2,1)} custom-call(s32[1,64]{1,0:T(1,128)} %bitcast.13, bf16[64,3072]{1,0:T(8,128)(2,1)} %x_hbm.1, bf16[3072,8192]{1,0:T(8,128)(2,1)} %wg_hbm.1, bf16[3072,8192]{1,0:T(8,128)(2,1)} %wu_hbm.1, bf16[8192,3072]{1,0:T(8,128)(2,1)} %wd_hbm.1, bf16[128,3072]{1,0:T(8,128)(2,1)} %bitcast.10, bf16[128,8192]{1,0:T(8,128)(2,1)} %bitcast.7, ...), custom_call_target="tpu_custom_call" | custom-call | tf_op jit(solution)/shard_map/lora_swiglu/pallas_call | solution.py:426
  64.5 1.8 %copy.13 = bf16[64,3072]{1,0:T(8,128)(2,1)} copy(bf16[64,3072]{1,0:T(8,128)(2,1)} %lora_swiglu.1) | data formatting | bytes 786432

commit v5 on v4

--- a/solution.py
+++ b/solution.py
@@ -31,7 +31,7 @@
     return lax.dot_general(a, b, (((1,), (1,)), ((), ())), preferred_element_type=F32)
 
 
-def layer(groups, cap, scale, rank, ids_ref, x_hbm, wg_hbm, wu_hbm, wd_hbm, ag_hbm, bg_hbm, au_hbm, bu_hbm, ad_hbm, bd_hbm, out_v,
+def layer(groups, cap, scale, rank, ids_ref, x_hbm, wg_hbm, wu_hbm, wd_hbm, ag_hbm, bg_hbm, au_hbm, bu_hbm, ad_hbm, bd_hbm, out_hbm,
           ring, acc_v, x_v, xc, h_v, bgu, adv, bdv, sendx, recvx, sendm, recvm, land, keep_v, low_v, gmat, unmap, remap,
           ring_sem, in_sem, s1_sem, r1_sem, s2_sem, land_sem, part_sem, free_sem):
     tok, dim = x_v.shape
@@ -99,9 +99,9 @@
         for r in order:
             pl.semaphore_signal(barrier, inc=1, device_id=target(r), device_id_type=pl.DeviceIdType.MESH)
 
-    early = [in_copy(ag_hbm, h_v.at[pl.ds(0, stack), pl.ds(0, dim)], 1), in_copy(au_hbm, h_v.at[pl.ds(0, stack), pl.ds(dim, dim)], 2),
-             in_copy(bg_hbm, bgu.at[0], 3), in_copy(bu_hbm, bgu.at[1], 4)]
-    late = [in_copy(ad_hbm, adv, 5), in_copy(bd_hbm, bdv, 6)]
+    early = [in_copy(ag_hbm, h_v.at[pl.ds(0, stack), pl.ds(0, dim)], 1), in_copy(au_hbm, h_v.at[pl.ds(0, stack), pl.ds(dim, dim)], 1),
+             in_copy(bg_hbm, bgu.at[0], 2), in_copy(bu_hbm, bgu.at[1], 2)]
+    late = [in_copy(ad_hbm, adv, 3), in_copy(bd_hbm, bdv, 4)]
 
     with jax.named_scope("place"):
         ids = ids_ref[...].astype(F32)
@@ -259,8 +259,9 @@
             arrive(n_pass)
             pl.semaphore_signal(free_sem, inc=1, device_id=device(0, 0, 1), device_id_type=pl.DeviceIdType.MESH)
             with jax.named_scope("low"):
-                for cp in early:
-                    cp.wait()
+                down = h_v.at[pl.ds(0, stack), pl.ds(0, 2 * dim)]
+                in_copy(down, down, 1).wait()
+                in_copy(bgu, bgu, 2).wait()
                 for i in range(2):
                     low_v[i] = pick(sum(dot_t(xc[:, k:k + UNIT_N], h_v[0:stack, i * dim + k:i * dim + k + UNIT_N]) for k in range(0, dim, UNIT_N)))
         start = p * (UNITS // 2) if n == 1 else 0
@@ -360,9 +361,11 @@
                 slabs = land[n]
         with jax.named_scope(f"home{n}"):
             part = dense(slabs)
-            out_v[:, n * UNIT_N:n * UNIT_N + MAIN] = dot(gmat[0], part).astype(BF)
+            x_v[:, n * UNIT_N:n * UNIT_N + MAIN] = dot(gmat[0], part).astype(BF)
             tail = sum(dot(gmat[1 + k], part[:, k * w:(k + 1) * w]) for k in range(third))
-            out_v[:, n * UNIT_N + MAIN:(n + 1) * UNIT_N] = tail.astype(BF)
+            x_v[:, n * UNIT_N + MAIN:(n + 1) * UNIT_N] = tail.astype(BF)
+        cols = pl.ds(n * UNIT_N, UNIT_N)
+        in_copy(x_v.at[:, cols], out_hbm.at[:, cols], 5).start()
 
     for n in range(n_out):
         base = n * k_out
@@ -398,6 +401,7 @@
         hand_on(n)
     for n in range(n_out):
         home(n)
+    in_copy(x_v, out_hbm, 5).wait()
     all_of(sendx.at[m, others], s2_sem.at[0], land_sem.at[0, 0]).wait_send()
     all_of(sendx.at[m, 0, 1], s2_sem.at[1], land_sem.at[0, 1]).wait_send()
     all_of(sendx.at[pl.ds(0, m), others], s2_sem.at[2], land_sem.at[0, 0]).wait_send()
@@ -427,7 +431,7 @@
             functools.partial(layer, groups, cap, LORA_ALPHA / rank, rank),
             out_shape=jax.ShapeDtypeStruct((tok, dim), BF),
             in_specs=[pl.BlockSpec(memory_space=pltpu.VMEM)] + [anyspec] * 10,
-            out_specs=pl.BlockSpec(memory_space=pltpu.VMEM),
+            out_specs=anyspec,
             scratch_shapes=[
                 pltpu.VMEM((UNITS, UNIT_K, UNIT_N), BF),
                 pltpu.VMEM((2, slots, ff), F32),
@@ -447,7 +451,7 @@
                 pltpu.VMEM((1 + cap // 2, tok, groups * slab), BF),
                 pltpu.VMEM((1 + cap // 2, slots, groups * slab), BF),
                 pltpu.VMEM((1 + cap // 2, groups * slab, slots), BF),
-                dma((UNITS // 8,)), dma((8,)), dma((2, 2)), dma((n_out, 2)), dma((4,)), dma((n_out, 2)), dma((n_out - 1,)), pltpu.SemaphoreType.REGULAR,
+                dma((UNITS // 8,)), dma((6,)), dma((2, 2)), dma((n_out - 1, 2)), dma((4,)), dma((n_out, 2)), dma((n_out - 1,)), pltpu.SemaphoreType.REGULAR,
             ],
             compiler_params=pltpu.CompilerParams(collective_id=0, has_side_effects=True, vmem_limit_bytes=67043328),
             name="lora_swiglu",

time: 66.4 us -> 66.3 us (level)
  no operation moved by 1% of the time
where the time goes in v5:
time: 66.3 us; the launch traced here: 66.1 us
  Pallas kernels  64.3 us (97%)
  local copies, waits for them, and re-layouts  1.77 us (3%)
    pallas_call x1, Pallas kernels, device_step(): pl.pallas_call(functools.partial(layer, groups, cap, LORA_ALPHA / rank, r...  64.3 us
    unnamed x1, local copies, waits for them, and re-layouts  1.77 us

profile of v5, /device:TPU:97, one launch (start us, length us, event | category | flops | bytes accessed | tf_op | source)
XLA Modules:
  0.0 66.1 jit_solution(17984740401682137259)
XLA Ops:
  0.0 64.3 %lora_swiglu.1 = bf16[64,3072]{1,0:T(8,128)(2,1)} custom-call(s32[1,64]{1,0:T(1,128)} %bitcast.13, bf16[64,3072]{1,0:T(8,128)(2,1)} %x_hbm.1, bf16[3072,8192]{1,0:T(8,128)(2,1)} %wg_hbm.1, bf16[3072,8192]{1,0:T(8,128)(2,1)} %wu_hbm.1, bf16[8192,3072]{1,0:T(8,128)(2,1)} %wd_hbm.1, bf16[128,3072]{1,0:T(8,128)(2,1)} %bitcast.10, bf16[128,8192]{1,0:T(8,128)(2,1)} %bitcast.7, ...), custom_call_target="tpu_custom_call" | custom-call | tf_op jit(solution)/shard_map/lora_swiglu/pallas_call | solution.py:430
  64.3 1.8 %copy.13 = bf16[64,3072]{1,0:T(8,128)(2,1)} copy(bf16[64,3072]{1,0:T(8,128)(2,1)} %lora_swiglu.1) | data formatting | bytes 786432
